TPU v7x, 256 devices: a whole 4x4x8 slice. The times are simulated.
256 devices in a mesh: graph: 16 (over z, y_lo), row: 16 (over y_hi, x, core).
Axes of the slice: x: 4, y: 4 (y_hi: 2, y_lo: 2; y = y_hi * 2 + y_lo), z: 8, core: 2. Of those that a mesh axis runs over, the one named last changes fastest.
Arguments:
- tiles: bfloat16 [16384, 256, 256], P(('graph', 'row')), parts along dimension 0, may hold values from -0.25 to 0.25
- tile_rows: int32 [16384], P(('graph', 'row')), parts along dimension 0, may hold values from 0 to 15
- tile_cols: int32 [16384], P(('graph', 'row')), parts along dimension 0, may hold values from 0 to 255, as said below
- tile_count: int32 [256], P(('graph', 'row')), parts along dimension 0, may hold values from 8 to 64, as said below
- seeds: float32 [32, 1048576], P(None, ('graph', 'row')), parts along dimension 1, may hold values from -6 to 6
- decay: float32 [32], replicated, may hold values from 0.8 to 1
Outputs:
- scores: float32 [32, 1048576], P(None, ('graph', 'row')), parts along dimension 1
There are 16 independent parts, one for each index of `graph`. A program takes and returns all parts, laid end to end along the dimension named above; an argument that names none is the same for every part. Nothing has to cross between parts.
Inputs may be any that keep to these rules, and one draw needn't show every extreme that they name: `tile_cols`: among the slots of one row panel, the tile columns that fall in the 16 tile rows of any one panel take at most 4 distinct values; in every draw the live slots of some panel take exactly 4 distinct tile columns of some one panel. Only the first tile_count slots of a panel are live; in every draw one panel has all 64 slots live.
All inputs are finite; a program needn't handle non-finite values.
Results may differ from a plain program's by a relative error of at most 0.0027.
Values may be sent and summed in bfloat16 or wider, within the bound.
A program may use at most 64 MiB of HBM per device.

v0:
```python
import jax
import jax.numpy as jnp
from jax import lax
from jax.sharding import PartitionSpec as P

TILE = 256
NEED = 4
ITERS = 3


def sent_to_all(x, axis):
    copies = jnp.broadcast_to(x, (lax.axis_size(axis), *x.shape))
    return lax.all_to_all(copies, axis, split_axis=0, concat_axis=0, tiled=True)


def of_everyone(x, axis):
    everything = sent_to_all(x, axis)
    return jnp.sum(everything, axis=0)


def per_device(tiles, tile_rows, tile_cols, tile_count, seeds, decay):
    count_of_slots = tiles.shape[0]
    seed_count = seeds.shape[0]
    blk_local = seeds.shape[1] // TILE
    panel_total = lax.axis_size("row")
    active_flag = jnp.arange(count_of_slots, dtype=jnp.int32) < tile_count[0]
    matches = tile_rows[:, None] == jnp.arange(blk_local, dtype=jnp.int32)[None, :]
    indicator_matrix = (matches & active_flag[:, None]).astype(jnp.float32)
    owner_of = tile_cols // blk_local
    local_of = tile_cols % blk_local
    owner_hit = owner_of[:, None] == jnp.arange(panel_total, dtype=jnp.int32)[None, :]
    local_match = local_of[:, None] == jnp.arange(blk_local, dtype=jnp.int32)[None, :]
    live_owner = (owner_hit & active_flag[:, None]).astype(jnp.int32)
    present = jnp.einsum("tq,tb->qb", live_owner, local_match.astype(jnp.int32)) > 0
    ranking = jnp.cumsum(present.astype(jnp.int32), axis=1) - 1
    rank_hit = present[:, :, None] & (
        ranking[:, :, None] == jnp.arange(NEED, dtype=jnp.int32)[None, None, :]
    )
    block_ids = jnp.arange(blk_local, dtype=jnp.int32)[None, :, None]
    wanted = jnp.sum(jnp.where(rank_hit, block_ids, 0), axis=1)
    asked = lax.all_to_all(wanted, "row", split_axis=0, concat_axis=0, tiled=True)
    asked_flat = asked.reshape(panel_total * NEED)
    slot_rank = ranking[owner_of, local_of]
    slot_place = jnp.clip(owner_of * NEED + slot_rank, 0, panel_total * NEED - 1)
    iterate = seeds
    for step in range(ITERS):
        rounded = iterate.astype(jnp.bfloat16)
        own_blocks = rounded.reshape(seed_count, blk_local, TILE)
        outgoing = jnp.take(own_blocks, asked_flat, axis=1).reshape(
            seed_count, panel_total, NEED * TILE
        )
        arrived = lax.all_to_all(outgoing, "row", split_axis=1, concat_axis=1, tiled=True)
        arrived = arrived.reshape(seed_count, panel_total * NEED, TILE)
        picked = jnp.take(arrived, slot_place, axis=1)
        block_products = jnp.einsum(
            "trc,stc->str", tiles, picked, preferred_element_type=jnp.float32
        )
        reduced_sum = jnp.einsum(
            "mv,emy->evy", indicator_matrix, block_products, precision=lax.Precision.HIGHEST
        )
        reduced_sum = reduced_sum.reshape(seed_count, blk_local * TILE)
        iterate = decay[:, None] * reduced_sum + seeds
    squares = of_everyone(jnp.sum(iterate * iterate, axis=1), "row")
    total_nodes = panel_total * iterate.shape[1]
    norm_value = jnp.sqrt(squares / total_nodes + 1e-06)
    return iterate / norm_value[:, None]


def solution(mesh):
    in_specs = (
        P(("graph", "row"), None, None),
        P(("graph", "row")),
        P(("graph", "row")),
        P(("graph", "row")),
        P(None, ("graph", "row")),
        P(),
    )
    out_specs = P(None, ("graph", "row"))
    return jax.shard_map(
        per_device, mesh=mesh, in_specs=in_specs, out_specs=out_specs, check_vma=False
    )
```

profile of v0, /device:TPU:1, one launch (start us, length us, event | category | flops | bytes accessed | tf_op | source)
XLA Modules:
  0.0 138.7 jit_solution(12599641336655567563)
XLA Ops:
  0.7 0.7 fusion.37
  1.3 0.2 fusion.43
  1.5 0.2 reduce_window_sum.11
  1.7 0.2 select_reduce_fusion
  1.9 0.7 copy.60
  2.6 8.4 %all-to-all-start = ((s32[16,1,4]{2,1,0:T(1,128)}), s32[16,1,4]{2,1,0:T(1,128)S(1)}, u32[]{:S(2)}, u32[]{:S(2)}) async-start(s32[16,1,4]{2,1,0:T(1,128)} %copy.60), calls=%async_computation | async-start | bytes 16384 | tf_op jit(solution)/shard_map/all_to_all | solution.py:41
  11.0 1.1 convert_element_type.15
  12.1 5.8 %all-to-all-done = s32[16,1,4]{2,1,0:T(1,128)S(1)} async-done(((s32[16,1,4]{2,1,0:T(1,128)}), s32[16,1,4]{2,1,0:T(1,128)S(1)}, u32[]{:S(2)}, u32[]{:S(2)}) %all-to-all-start) | async-done | bytes 288 | tf_op jit(solution)/shard_map/all_to_all | solution.py:41
  17.9 0.5 broadcast.175
  18.4 0.7 reduce.4
  19.1 0.1 reshape.74
  19.2 0.6 gather_fusion.1
  19.9 0.2 select_bitcast_fusion.2
  20.0 0.6 copy.62
  20.6 0.7 reshape.75
  21.3 1.6 %copy.63 = bf16[32,16,1024]{2,0,1:T(8,128)(2,1)} copy(bf16[32,16,1024]{2,1,0:T(8,128)(2,1)S(1)} %reshape.75) | data formatting | bytes 2097152 | tf_op jit(solution)/shard_map/reshape | solution.py:49
  22.9 4.1 %all-to-all-start.1 = ((bf16[32,16,1024]{2,0,1:T(8,128)(2,1)}), bf16[32,16,1024]{2,0,1:T(8,128)(2,1)S(1)}, u32[]{:S(2)}, u32[]{:S(2)}) async-start(bf16[32,16,1024]{2,0,1:T(8,128)(2,1)} %copy.63), calls=%async_computation.1 | async-start | bytes 2097152 | tf_op jit(solution)/shard_map/all_to_all | solution.py:52
  27.0 0.8 gather_fusion
  27.8 16.5 %all-to-all-done.1 = bf16[32,16,1024]{2,0,1:T(8,128)(2,1)S(1)} async-done(((bf16[32,16,1024]{2,0,1:T(8,128)(2,1)}), bf16[32,16,1024]{2,0,1:T(8,128)(2,1)S(1)}, u32[]{:S(2)}, u32[]{:S(2)}) %all-to-all-start.1) | async-done | bytes 1048608 | tf_op jit(solution)/shard_map/all_to_all | solution.py:52
  44.4 0.6 copy.64
  44.9 0.7 reshape.76
  45.6 0.6 copy.65
  46.2 0.6 gather_fusion.2
  46.8 0.0 copy-start.2
  46.8 5.9 %convolution_bitcast_fusion.2 = f32[32,64,256]{2,0,1:T(8,128)S(1)} fusion(bf16[64,256,256]{2,1,0:T(8,128)(2,1)} %param.10, bf16[64,32,256]{2,1,0:T(8,128)(2,1)S(1)} %gather_fusion.2, pred[64]{0:T(512)(128)(4,1)S(1)} %get-tuple-element.6), kind=kOutput, calls=%fused_computation.15 | convolution fusion | flops 268959744 | bytes 11534400 | tf_op jit(solution)/shard_map/trc,stc->str/dot_general | solution.py:55
  52.8 0.0 copy-done.2
  52.8 0.0 copy-start
  52.8 0.0 copy-start.1
  52.8 2.0 %fusion.4 = f32[32,256,16]{1,2,0:T(8,128)S(1)} fusion(f32[32,64,256]{2,0,1:T(8,128)S(1)} %convolution_bitcast_fusion.2, s32[64]{0:T(128)S(1)} %copy-done.2, pred[64]{0:T(512)(128)(4,1)S(1)} %iota_compare_fusion.5), kind=kOutput, calls=%fused_computation.11 | convolution fusion | flops 100665344 | bytes 2621760 | tf_op jit(solution)/shard_map/mv,emy->evy/dot_general | solution.py:58
  54.8 0.3 copy.83
  55.1 0.0 copy-done
  55.1 0.0 copy-done.1
  55.1 0.1 add_convert_fusion.1
  55.3 0.6 gather_fusion.3
  55.9 0.2 select_bitcast_fusion.1
  56.1 0.6 copy.68
  56.6 0.7 reshape.79
  57.3 0.6 copy.69
  57.9 19.9 %all_to_all.30 = bf16[32,16,1024]{2,0,1:T(8,128)(2,1)S(1)} all-to-all(bf16[32,16,1024]{2,0,1:T(8,128)(2,1)S(1)} %copy.69), channel_id=1, replica_groups=mesh['graph'=16,'row'=16] {'row'}, dimensions={1} | all-to-all | bytes 2097152 | tf_op jit(solution)/shard_map/all_to_all | solution.py:52
  77.8 0.6 copy.70
  78.4 1.5 %reshape.80 = bf16[32,64,256]{2,1,0:T(8,128)(2,1)} reshape(bf16[32,16,1024]{2,1,0:T(8,128)(2,1)S(1)} %copy.70) | data formatting | bytes 2097152 | tf_op jit(solution)/shard_map/reshape | solution.py:53
  79.9 1.8 %copy.71 = bf16[32,64,256]{2,0,1:T(8,128)(2,1)S(1)} copy(bf16[32,64,256]{2,1,0:T(8,128)(2,1)} %reshape.80) | data formatting | bytes 2097152 | tf_op jit(solution)/shard_map/reshape | solution.py:53
  81.7 0.6 gather_fusion.4
  82.3 5.9 %convolution_bitcast_fusion.1 = f32[32,64,256]{2,0,1:T(8,128)S(1)} fusion(bf16[64,256,256]{2,1,0:T(8,128)(2,1)} %param.10, bf16[64,32,256]{2,1,0:T(8,128)(2,1)S(1)} %gather_fusion.4, pred[64]{0:T(512)(128)(4,1)S(1)} %get-tuple-element.6), kind=kOutput, calls=%fused_computation.14 | convolution fusion | flops 268959744 | bytes 11534400 | tf_op jit(solution)/shard_map/trc,stc->str/dot_general | solution.py:55
  88.2 2.0 %fusion.2 = f32[32,256,16]{1,2,0:T(8,128)S(1)} fusion(f32[32,64,256]{2,0,1:T(8,128)S(1)} %convolution_bitcast_fusion.1, s32[64]{0:T(128)S(1)} %copy-done.2, pred[64]{0:T(512)(128)(4,1)S(1)} %iota_compare_fusion.5), kind=kOutput, calls=%fused_computation.9 | convolution fusion | flops 100665344 | bytes 2621760 | tf_op jit(solution)/shard_map/mv,emy->evy/dot_general | solution.py:58
  90.2 0.3 copy.84
  90.5 0.1 add_convert_fusion
  90.7 0.6 gather_fusion.5
  91.3 0.2 select_bitcast_fusion
  91.5 0.6 copy.74
  92.1 0.7 reshape.83
  92.7 0.6 copy.75
  93.3 20.6 %all_to_all.31 = bf16[32,16,1024]{2,0,1:T(8,128)(2,1)S(1)} all-to-all(bf16[32,16,1024]{2,0,1:T(8,128)(2,1)S(1)} %copy.75), channel_id=1, replica_groups=mesh['graph'=16,'row'=16] {'row'}, dimensions={1} | all-to-all | bytes 2097152 | tf_op jit(solution)/shard_map/all_to_all | solution.py:52
  113.9 0.6 copy.76
  114.5 1.5 %reshape.84 = bf16[32,64,256]{2,1,0:T(8,128)(2,1)} reshape(bf16[32,16,1024]{2,1,0:T(8,128)(2,1)S(1)} %copy.76) | data formatting | bytes 2097152 | tf_op jit(solution)/shard_map/reshape | solution.py:53
  116.0 1.8 %copy.77 = bf16[32,64,256]{2,0,1:T(8,128)(2,1)S(1)} copy(bf16[32,64,256]{2,1,0:T(8,128)(2,1)} %reshape.84) | data formatting | bytes 2097152 | tf_op jit(solution)/shard_map/reshape | solution.py:53
  117.8 0.6 gather_fusion.6
  118.4 5.9 %convolution_bitcast_fusion = f32[32,64,256]{2,0,1:T(8,128)S(1)} fusion(bf16[64,256,256]{2,1,0:T(8,128)(2,1)} %param.10, bf16[64,32,256]{2,1,0:T(8,128)(2,1)S(1)} %gather_fusion.6, pred[64]{0:T(512)(128)(4,1)S(1)} %get-tuple-element.6), kind=kOutput, calls=%fused_computation.13 | convolution fusion | flops 268959744 | bytes 11534400 | tf_op jit(solution)/shard_map/trc,stc->str/dot_general | solution.py:55
  124.3 2.0 %fusion = f32[32,256,16]{1,2,0:T(8,128)S(1)} fusion(f32[32,64,256]{2,0,1:T(8,128)S(1)} %convolution_bitcast_fusion, s32[64]{0:T(128)S(1)} %copy-done.2, pred[64]{0:T(512)(128)(4,1)S(1)} %iota_compare_fusion.5), kind=kOutput, calls=%fused_computation.7 | convolution fusion | flops 100665344 | bytes 2621760 | tf_op jit(solution)/shard_map/mv,emy->evy/dot_general | solution.py:58
  126.3 0.3 copy.85
  126.6 0.3 multiply_reduce_fusion
  126.9 10.9 %all_to_all.32 = f32[16,1,32]{2,1,0:T(1,128)S(1)} all-to-all(f32[16,1,32]{2,1,0:T(1,128)S(1)} %broadcast_in_dim.59), channel_id=1, replica_groups=mesh['graph'=16,'row'=16] {'row'}, dimensions={0} | all-to-all | bytes 4096 | tf_op jit(solution)/shard_map/all_to_all | solution.py:13
  137.8 0.9 broadcast_divide_fusion
  (13 shorter events, 0.1 us)
Async XLA Ops:
  2.6 15.4 %all-to-all-start = ((s32[16,1,4]{2,1,0:T(1,128)}), s32[16,1,4]{2,1,0:T(1,128)S(1)}, u32[]{:S(2)}, u32[]{:S(2)}) async-start(s32[16,1,4]{2,1,0:T(1,128)} %copy.60), calls=%async_computation | async-start | bytes 16384 | tf_op jit(solution)/shard_map/all_to_all | solution.py:41
  22.9 21.5 %all-to-all-start.1 = ((bf16[32,16,1024]{2,0,1:T(8,128)(2,1)}), bf16[32,16,1024]{2,0,1:T(8,128)(2,1)S(1)}, u32[]{:S(2)}, u32[]{:S(2)}) async-start(bf16[32,16,1024]{2,0,1:T(8,128)(2,1)} %copy.63), calls=%async_computation.1 | async-start | bytes 2097152 | tf_op jit(solution)/shard_map/all_to_all | solution.py:52
  46.8 5.9 %copy-start.2 = (s32[64]{0:T(128)S(1)}, s32[64]{0:T(128)}, u32[]{:S(2)}) copy-start(s32[64]{0:T(128)} %param.11) | copy-start | bytes 772
  52.8 2.3 %copy-start = (f32[32,4096]{1,0:T(8,128)S(1)}, f32[32,4096]{1,0:T(8,128)}, u32[]{:S(2)}) copy-start(f32[32,4096]{1,0:T(8,128)} %param.14) | copy-start | bytes 1572868
  52.8 2.3 %copy-start.1 = (f32[32]{0:T(128)S(1)}, f32[32]{0:T(128)}, u32[]{:S(2)}) copy-start(f32[32]{0:T(128)} %param.15) | copy-start | bytes 388
where the time goes:
time: 139 us
  blocking collectives  51.4 us (37%)
  matrix products  23.8 us (17%)
  local copies, waits for them, and re-layouts  22.8 us (16%)
  waiting for transfers between devices  22.4 us (16%)
  starting transfers between devices  12.5 us (9%)
  other arithmetic  4.73 us (3%)
    all_to_all x2, blocking collectives, per_device(): lax.all_to_all(outgoing, 'row', split_axis=1, concat_axis=1, tiled=True)  40.5 us
    dot_general x3, matrix products, per_device(): jnp.einsum('trc,stc->str', tiles, picked, preferred_element_type=jnp.floa...  17.7 us
    all_to_all x1, waiting for transfers between devices, per_device(): lax.all_to_all(outgoing, 'row', split_axis=1, concat_axis=1, tiled=True)  16.5 us
    all_to_all x1, blocking collectives, sent_to_all(): return lax.all_to_all(copies, axis, split_axis=0, concat_axis=0, tiled=True)  10.9 us
    all_to_all x1, starting transfers between devices, per_device(): lax.all_to_all(wanted, 'row', split_axis=0, concat_axis=0, tiled=True)  8.44 us
    reshape x6, local copies, waits for them, and re-layouts, per_device(): arrived = arrived.reshape(seed_count, panel_total * NEED, TILE)  7.81 us
    dot_general x3, matrix products, per_device(): jnp.einsum('mv,emy->evy', indicator_matrix, block_products, precision=lax...  5.89 us
    all_to_all x1, waiting for transfers between devices, per_device(): lax.all_to_all(wanted, 'row', split_axis=0, concat_axis=0, tiled=True)  5.84 us
  transfers between devices with their start and end apart: 2, of which 2 were waited for; matrix products, arithmetic and copies ran while one was open for 1% of the time, Pallas kernels for 0%

commit v1 on v0

v1 whole, which is shorter than its diff:
```python
import functools

import jax
import jax.numpy as jnp
from jax import lax
from jax.experimental import pallas as pl
from jax.experimental.pallas import tpu as pltpu
from jax.sharding import PartitionSpec as P

TILE = 256
NEED = 4
ITERS = 3
HALVES = 2
MESH = pl.DeviceIdType.MESH
NEG = [(d // 8) * 8 + ((4 - (d // 2) % 4) % 4) * 2 + d % 2 for d in range(16)]


def hops(d):
    dx = (d // 2) % 4
    return min(dx, 4 - dx) + 2 * (d // 8)


FAR = sorted(range(1, 16), key=lambda d: (-hops(d), d))


def kernel(
    tiles_hbm, rows_ref, cols_ref, count_ref, seeds_hbm, decay_ref,
    out_hbm, norm_ref,
    tiles, tiles_t, seeds, own, sendbuf,
    recv0, recv1, recv2, recv3, recv4, recv5, pref, res,
    meta_out, meta_in, meta_sm, tab, tab_sm, sq_out, sq_in,
    load_sem, tab_sem, self_sem, meta_ssem, meta_rsem, asm_sem,
    ssem, rsem, sq_ssem, sq_rsem, out_sem,
):
    slots = tiles.shape[0]
    n_row = 16
    blk = 16
    recv = [recv0, recv1, recv2, recv3, recv4, recv5]
    phases = ITERS * HALVES
    half = seeds.shape[0] // HALVES
    me = lax.axis_index("row")
    my_y, my_x, my_c = me // 8, lax.rem(me // 2, 4), lax.rem(me, 2)

    def peer(d):
        py = lax.rem(my_y + d // 8, 2)
        px = lax.rem(my_x + (d // 2) % 4, 4)
        pc = lax.rem(my_c + d % 2, 2)
        return {"row": py * 8 + px * 2 + pc}

    def bounded(i, n):
        return jnp.minimum(jnp.maximum(i, 0), n - 1)

    barrier = pltpu.get_barrier_semaphore()
    for d in FAR:
        pl.semaphore_signal(barrier, inc=1, device_id=peer(d), device_id_type=MESH)

    seed_load = pltpu.make_async_copy(seeds_hbm, seeds, load_sem.at[8])
    seed_load.start()
    part = slots // 8
    tile_loads = [
        pltpu.make_async_copy(tiles_hbm.at[pl.ds(i * part, part)], tiles.at[pl.ds(i * part, part)], load_sem.at[i])
        for i in range(8)
    ]
    for copy in tile_loads:
        copy.start()

    f32 = jnp.float32
    i32 = jnp.int32

    def iota(shape, axis):
        return lax.broadcasted_iota(i32, shape, axis)

    def total(hit, v, axis):
        return jnp.sum(jnp.where(hit, v, 0), axis=axis, keepdims=True)

    ncol = n_row * blk
    cols_l = cols_ref[...]
    live_l = iota((1, slots), 1) < count_ref[...]
    key_l = jnp.where(live_l, rows_ref[...], blk)
    sub = iota((slots, slots), 0)
    lane = iota((slots, slots), 1)
    cols_s = total(sub == lane, cols_l, 1)
    key_s = total(sub == lane, key_l, 1)
    before = (key_l == key_s) & (lane < sub)
    pos_s = total((key_l < key_s) | before, 1, 1)
    keep_s = jnp.minimum(total(before, 1, 1), 1)
    place_hot = pos_s == lane

    present_s = jnp.minimum(total((cols_l == iota((ncol, slots), 0)) & live_l, 1, 1), 1)
    c_a = iota((ncol, ncol), 0)
    c_b = iota((ncol, ncol), 1)
    rank_l = total((c_a // blk == c_b // blk) & (c_a < c_b), present_s, 0)
    present_l = total(c_a == c_b, present_s, 0)
    c_l = iota((1, ncol), 1)
    owner = c_l // blk
    slot_l = (
        ((my_y + 2 - owner // 8) % 2) * 8
        + ((my_x + 4 - (owner // 2) % 4) % 4) * 2
        + (my_c + 2 - owner % 2) % 2
    )
    place_l = slot_l * NEED + jnp.minimum(rank_l, NEED - 1)
    place_s = total(cols_s == c_l, place_l, 1)
    mine = (slot_l == iota((16, ncol), 0)) & (present_l > 0)
    wanted = jnp.zeros((16, 128), i32)
    for k in range(NEED):
        pick = total(mine & (rank_l == k), c_l % blk, 1)
        wanted = jnp.where(iota((16, 128), 1) == k, pick, wanted)
    for d in range(16):
        meta_out[d] = wanted[d:d + 1, :]

    slot_id = iota((slots, 1), 0)
    tab[0:1, 0:slots] = total(place_hot, slot_id, 0)
    tab[1:2, 0:slots] = total(place_hot, place_s, 0)
    tab[2:3, 0:slots] = total(place_hot, keep_s, 0)
    upto = total(key_s <= lane, 1, 0)
    tab[3:4, 0:slots] = jnp.maximum(upto - 1, 0)
    tab[4:5, 0:slots] = total(key_s == lane, 1, 0)

    tab_copy = pltpu.make_async_copy(tab, tab_sm, tab_sem)
    tab_copy.start()
    self_copy = pltpu.make_async_copy(meta_out.at[0], meta_sm.at[0], self_sem)
    self_copy.start()

    pl.semaphore_wait(barrier, n_row - 1)

    def request(d):
        return pltpu.make_async_remote_copy(
            src_ref=meta_out.at[d], dst_ref=meta_in.at[d],
            send_sem=meta_ssem.at[d], recv_sem=meta_rsem.at[d],
            device_id=peer(NEG[d]), device_id_type=MESH,
        )

    for d in FAR:
        request(d).start()

    decay_l = decay_ref[...]
    nseed = seeds.shape[0]
    e_sub = lax.broadcasted_iota(i32, (nseed, nseed), 0)
    e_lane = lax.broadcasted_iota(i32, (nseed, nseed), 1)
    decay = jnp.sum(jnp.where(e_sub == e_lane, decay_l, 0.0), axis=1, keepdims=True)
    res[0:nseed, 0:128] = jnp.broadcast_to(decay, (nseed, 128))

    seed_load.wait()
    tab_copy.wait()
    self_copy.wait()

    def exchange(p, d):
        return pltpu.make_async_remote_copy(
            src_ref=sendbuf.at[p, pl.ds(d * NEED, NEED)], dst_ref=recv[p].at[pl.ds(d * NEED, NEED)],
            send_sem=ssem.at[p, d], recv_sem=rsem.at[p, d],
            device_id=peer(d), device_id_type=MESH,
        )

    def fill(p, d):
        for k in range(NEED):
            sendbuf[p, d * NEED + k] = own[p, bounded(meta_sm[d, 0, k], blk)]

    def fill_self(p):
        for k in range(NEED):
            recv[p][k] = own[p, bounded(meta_sm[0, 0, k], blk)]

    for h in range(HALVES):
        for r in range(blk):
            own[h, r] = seeds[h * half:(h + 1) * half, r * TILE:(r + 1) * TILE].astype(jnp.bfloat16)
    near = FAR[::-1]
    for d in near:
        request(d).wait_recv()
        to_sm = pltpu.make_async_copy(meta_in.at[d], meta_sm.at[d], asm_sem.at[d])
        to_sm.start()
    for d in near:
        pltpu.make_async_copy(meta_in.at[d], meta_sm.at[d], asm_sem.at[d]).wait()
    for p in range(HALVES):
        last = None
        for d in FAR:
            fill(p, d)
            if last is not None:
                exchange(p, last).start()
            last = d
        fill_self(p)
        exchange(p, last).start()
    for copy in tile_loads:
        copy.wait()

    def turn(i, _):
        tiles_t[i] = tiles[bounded(tab_sm[0, i], slots)].T
        return 0

    lax.fori_loop(0, slots, turn, 0, unroll=4)
    for d in FAR:
        request(d).wait_send()

    group = 16

    def phase(p):
        h = p % HALVES
        for d in FAR:
            exchange(p, d).wait_recv()

        def tiles_step(g, acc):
            for u in range(group):
                i = g * group + u
                product = jnp.dot(recv[p][bounded(tab_sm[1, i], n_row * NEED)], tiles_t[i], preferred_element_type=f32)
                acc = jnp.where(tab_sm[2, i] > 0, acc, 0.0) + product
                pref[i] = acc
            return acc

        lax.fori_loop(0, slots // group, tiles_step, jnp.zeros((half, TILE), f32))
        rows_h = pl.ds(h * half, half)
        gain = res[rows_h, 0:1]

        def value(r):
            reach = jnp.where(tab_sm[4, r] > 0, pref[bounded(tab_sm[3, r], slots)], 0.0)
            return gain * reach + seeds[rows_h, r * TILE:(r + 1) * TILE]

        if p < phases - HALVES:
            nxt = p + HALVES
            for r in range(blk):
                own[nxt, r] = value(r).astype(jnp.bfloat16)
            last = None
            for d in FAR:
                fill(nxt, d)
                if last is not None:
                    exchange(nxt, last).start()
                last = d
            fill_self(nxt)
            exchange(nxt, last).start()

        else:
            square = jnp.zeros((half, TILE), f32)
            for r in range(blk):
                v = value(r)
                res[rows_h, 128 + r * TILE:128 + (r + 1) * TILE] = v
                square = square + v * v
            energy = jnp.sum(square, axis=1, keepdims=True)
            q_sub = lax.broadcasted_iota(i32, (half, 128), 0)
            q_lane = lax.broadcasted_iota(i32, (half, 128), 1)
            flat = jnp.sum(jnp.where(q_sub == q_lane, energy, 0.0), axis=0, keepdims=True)
            sq_out[h] = flat
            sq_in[h, 0] = flat
            for d in FAR:
                squares(h, d).start()
            pltpu.make_async_copy(
                res.at[rows_h, pl.ds(128, blk * TILE)], out_hbm.at[rows_h, :], out_sem.at[h]
            ).start()

        for d in FAR:
            exchange(p, d).wait_send()

    def squares(h, d):
        return pltpu.make_async_remote_copy(
            src_ref=sq_out.at[h], dst_ref=sq_in.at[h, d],
            send_sem=sq_ssem.at[h, d], recv_sem=sq_rsem.at[h, d],
            device_id=peer(d), device_id_type=MESH,
        )

    for p in range(phases):
        phase(p)
    for h in range(HALVES):
        for d in FAR:
            squares(h, d).wait()
    for h in range(HALVES):
        acc = sq_in[h, 0]
        for d in range(1, 16):
            acc = acc + sq_in[h, d]
        norm_ref[h:h + 1, :] = acc
    for h in range(HALVES):
        pltpu.make_async_copy(
            res.at[pl.ds(h * half, half), pl.ds(128, blk * TILE)],
            out_hbm.at[pl.ds(h * half, half), :], out_sem.at[h],
        ).wait()


def per_device(tiles, tile_rows, tile_cols, tile_count, seeds, decay):
    slots = tiles.shape[0]
    nseed, width = seeds.shape
    blk = width // TILE
    n_row = lax.axis_size("row")
    half = nseed // HALVES
    phases = ITERS * HALVES
    bf16, f32, i32 = jnp.bfloat16, jnp.float32, jnp.int32
    vmem = pl.BlockSpec(memory_space=pltpu.VMEM)
    anywhere = pl.BlockSpec(memory_space=pl.ANY)
    dma = pltpu.SemaphoreType.DMA
    iterate, squares = pl.pallas_call(
        kernel,
        out_shape=(
            jax.ShapeDtypeStruct((nseed, width), f32),
            jax.ShapeDtypeStruct((HALVES, 128), f32),
        ),
        in_specs=[anywhere, vmem, vmem, vmem, anywhere, vmem],
        out_specs=(anywhere, vmem),
        scratch_shapes=[
            pltpu.VMEM((slots, TILE, TILE), bf16),
            pltpu.VMEM((slots, TILE, TILE), bf16),
            pltpu.VMEM((nseed, width), f32),
            pltpu.VMEM((phases, blk, half, TILE), bf16),
            pltpu.VMEM((phases, n_row * NEED, half, TILE), bf16),
            *[pltpu.VMEM((n_row * NEED, half, TILE), bf16) for _ in range(phases)],
            pltpu.VMEM((slots, half, TILE), f32),
            pltpu.VMEM((nseed, 128 + width), f32),
            pltpu.VMEM((16, 1, 128), i32),
            pltpu.VMEM((16, 1, 128), i32),
            pltpu.SMEM((16, 1, 128), i32),
            pltpu.VMEM((8, 128), i32),
            pltpu.SMEM((8, 128), i32),
            pltpu.VMEM((HALVES, 1, 128), f32),
            pltpu.VMEM((HALVES, 16, 1, 128), f32),
            dma((9,)), dma, dma, dma((16,)), dma((16,)), dma((16,)),
            dma((phases, 16)), dma((phases, 16)), dma((HALVES, 16)), dma((HALVES, 16)), dma((HALVES,)),
        ],
        compiler_params=pltpu.CompilerParams(collective_id=0, has_side_effects=True),
        name="katz",
    )(
        tiles, tile_rows.reshape(1, slots), tile_cols.reshape(1, slots),
        tile_count.reshape(1, 1), seeds, decay.reshape(1, nseed),
    )
    total_nodes = n_row * width
    norm_value = jnp.sqrt(squares[:, :half].reshape(nseed) / total_nodes + 1e-06)
    return iterate / norm_value[:, None]


def solution(mesh):
    in_specs = (
        P(("graph", "row"), None, None),
        P(("graph", "row")),
        P(("graph", "row")),
        P(("graph", "row")),
        P(None, ("graph", "row")),
        P(),
    )
    out_specs = P(None, ("graph", "row"))
    return jax.shard_map(
        per_device, mesh=mesh, in_specs=in_specs, out_specs=out_specs, check_vma=False
    )
```

time: 139 us -> 62.6 us (0.45)
  Pallas kernels: 0 us -> 58.9 us
  blocking collectives: 51.4 us -> 0 us
  matrix products: 23.8 us -> 0 us
  local copies, waits for them, and re-layouts: 22.8 us -> 0.08 us
  waiting for transfers between devices: 22.4 us -> 0 us
  starting transfers between devices: 12.5 us -> 0 us
  other arithmetic: 4.73 us -> 2.59 us
    pallas_call x0 -> x1, Pallas kernels: none -> 58.9 us  [per_device(): pl.pallas_call(kernel, out_shape=(jax.ShapeDtypeStruct((nseed, width), f3...]
    all_to_all x3 -> x0, blocking collectives: 51.4 us -> none  [the longest x2 40.5 us: per_device(): lax.all_to_all(outgoing, 'row', split_axis=1, concat_axis=1, tiled=True)]
    dot_general x7 -> x0, matrix products: 23.8 us -> none  [the longest x3 17.7 us: per_device(): jnp.einsum('trc,stc->str', tiles, picked, preferred_element_type=jnp.floa...]
    all_to_all x2 -> x0, waiting for transfers between devices: 22.4 us -> none  [the longest x1 16.5 us: per_device(): lax.all_to_all(outgoing, 'row', split_axis=1, concat_axis=1, tiled=True)]
    reshape x16 -> x0, local copies, waits for them, and re-layouts: 12.7 us -> none  [the longest x6 7.81 us: per_device(): arrived = arrived.reshape(seed_count, panel_total * NEED, TILE)]
    all_to_all x2 -> x0, starting transfers between devices: 12.5 us -> none  [the longest x1 8.44 us: per_device(): lax.all_to_all(wanted, 'row', split_axis=0, concat_axis=0, tiled=True)]
    gather x7 -> x0, local copies, waits for them, and re-layouts: 4.49 us -> none  [the longest x3 1.85 us: per_device(): jnp.take(own_blocks, asked_flat, axis=1)]
    all_to_all x5 -> x0, local copies, waits for them, and re-layouts: 2.94 us -> none  [the longest x3 1.74 us: per_device(): lax.all_to_all(outgoing, 'row', split_axis=1, concat_axis=1, tiled=True)]
  transfers between devices with their start and end apart: 2 -> 0, of which waited for: 2 -> 0; matrix products, arithmetic and copies ran while one was open for 1% -> 0% of each run, Pallas kernels for 0% -> 0%
where the time goes in v1:
time: 62.6 us; the launch traced here: 62.3 us
  Pallas kernels  58.9 us (94%)
  other arithmetic  2.59 us (4%)
  between operations  0.66 us (1%)
    pallas_call x1, Pallas kernels, per_device(): pl.pallas_call(kernel, out_shape=(jax.ShapeDtypeStruct((nseed, width), f3...  58.9 us
    div x1, other arithmetic, per_device(): return iterate / norm_value[:, None]  1.95 us

profile of v1, /device:TPU:1, one launch (start us, length us, event | category | flops | bytes accessed | tf_op | source)
XLA Modules:
  0.0 62.3 jit_solution(13174445812319904277)
XLA Ops:
  0.7 58.9 %katz.1 = (f32[32,4096]{1,0:T(8,128)}, f32[2,128]{1,0:T(2,128)}) custom-call(bf16[64,256,256]{2,1,0:T(8,128)(2,1)} %tiles_hbm.1, s32[1,64]{1,0:T(1,128)} %bitcast.5, s32[1,64]{1,0:T(1,128)} %bitcast.6, s32[1,1]{1,0:T(1,128)} %bitcast.4.count_ref, f32[32,4096]{1,0:T(8,128)} %seeds_hbm.1, f32[1,32]{1,0:T(1,128)} %bitcast.7), custom_call_target="tpu_custom_call" | custom-call | tf_op jit(solution)/shard_map/katz/pallas_call | solution.py:284
  59.6 0.6 %add_sqrt_fusion = f32[2,16]{1,0:T(2,128)S(1)} fusion(f32[2,128]{1,0:T(2,128)} %get-tuple-element.8), kind=kLoop, calls=%fused_computation.1 | loop fusion | flops 64 | bytes 256 | tf_op jit(solution)/shard_map/sqrt | solution.py:318
  60.2 0.1 sqrt.11
  60.3 1.9 %broadcast_divide_fusion = f32[32,4096]{1,0:T(8,128)} fusion(f32[32,4096]{1,0:T(8,128)} %get-tuple-element.7, f32[32]{0:T(128)S(1)} %sqrt.11), kind=kLoop, calls=%fused_computation | loop fusion | flops 131072 | bytes 1048704 | tf_op jit(solution)/shard_map/div | solution.py:319

commit v2 on v1

--- a/solution.py
+++ b/solution.py
@@ -24,13 +24,13 @@
 
 
 def kernel(
-    tiles_hbm, rows_ref, cols_ref, count_ref, seeds_hbm, decay_ref,
-    out_hbm, norm_ref,
+    tiles_hbm, rows_hbm, cols_hbm, count_ref, seeds_hbm, decay_hbm,
+    out_ref,
     tiles, tiles_t, seeds, own, sendbuf,
     recv0, recv1, recv2, recv3, recv4, recv5, pref, res,
-    meta_out, meta_in, meta_sm, tab, tab_sm, sq_out, sq_in,
-    load_sem, tab_sem, self_sem, meta_ssem, meta_rsem, asm_sem,
-    ssem, rsem, sq_ssem, sq_rsem, out_sem,
+    rows_v, cols_v, decay_v, meta_out, meta_sm, tab, tab_sm, sq_out, sq_in,
+    load_sem, tab_sem, self_sem, meta_ssem, meta_rsem,
+    ssem, rsem, sq_ssem, sq_rsem,
 ):
     slots = tiles.shape[0]
     n_row = 16
@@ -54,6 +54,12 @@
     for d in FAR:
         pl.semaphore_signal(barrier, inc=1, device_id=peer(d), device_id_type=MESH)
 
+    small_loads = [
+        pltpu.make_async_copy(src, dst, load_sem.at[9 + i])
+        for i, (src, dst) in enumerate(((cols_hbm, cols_v), (rows_hbm, rows_v), (decay_hbm, decay_v)))
+    ]
+    for copy in small_loads:
+        copy.start()
     seed_load = pltpu.make_async_copy(seeds_hbm, seeds, load_sem.at[8])
     seed_load.start()
     part = slots // 8
@@ -64,6 +70,8 @@
     for copy in tile_loads:
         copy.start()
 
+    for copy in small_loads:
+        copy.wait()
     f32 = jnp.float32
     i32 = jnp.int32
 
@@ -74,40 +82,55 @@
         return jnp.sum(jnp.where(hit, v, 0), axis=axis, keepdims=True)
 
     ncol = n_row * blk
-    cols_l = cols_ref[...]
-    live_l = iota((1, slots), 1) < count_ref[...]
-    key_l = jnp.where(live_l, rows_ref[...], blk)
+    cols_l = cols_v[...]
+    live_l = iota((1, slots), 1) < count_ref[0]
+    key_l = jnp.where(live_l, rows_v[...], blk)
     sub = iota((slots, slots), 0)
     lane = iota((slots, slots), 1)
     cols_s = total(sub == lane, cols_l, 1)
+    present_s = jnp.minimum(total((cols_l == iota((ncol, slots), 0)) & live_l, 1, 1), 1)
+    c_a = iota((ncol, ncol), 0)
+    c_b = iota((ncol, ncol), 1)
+    rank_l = total(((c_a >> 4) == (c_b >> 4)) & (c_a < c_b), present_s, 0)
+    present_l = total(c_a == c_b, present_s, 0)
+    c_l = iota((1, ncol), 1)
+    owner = c_l >> 4
+    slot_l = (
+        ((my_y + 2 - (owner >> 3)) & 1) * 8
+        + ((my_x + 4 - ((owner >> 1) & 3)) & 3) * 2
+        + ((my_c + 2 - owner) & 1)
+    )
+    place_l = slot_l * NEED + jnp.minimum(rank_l, NEED - 1)
+    mine = (slot_l == iota((16, ncol), 0)) & (present_l > 0)
+    wanted = jnp.zeros((16, 128), i32)
+    for k in range(NEED):
+        pick = total(mine & (rank_l == k), c_l & 15, 1)
+        wanted = jnp.where(iota((16, 128), 1) == k, pick, wanted)
+    for d in range(16):
+        meta_out[d] = wanted[d:d + 1, :]
+
+    self_copy = pltpu.make_async_copy(meta_out.at[0], meta_sm.at[0], self_sem)
+    self_copy.start()
+
+    pl.semaphore_wait(barrier, n_row - 1)
+
+    def request(d):
+        return pltpu.make_async_remote_copy(
+            src_ref=meta_out.at[d], dst_ref=meta_sm.at[d],
+            send_sem=meta_ssem.at[d], recv_sem=meta_rsem.at[d],
+            device_id=peer(NEG[d]), device_id_type=MESH,
+        )
+
+    for d in FAR:
+        request(d).start()
+
     key_s = total(sub == lane, key_l, 1)
     before = (key_l == key_s) & (lane < sub)
     pos_s = total((key_l < key_s) | before, 1, 1)
     keep_s = jnp.minimum(total(before, 1, 1), 1)
     place_hot = pos_s == lane
 
-    present_s = jnp.minimum(total((cols_l == iota((ncol, slots), 0)) & live_l, 1, 1), 1)
-    c_a = iota((ncol, ncol), 0)
-    c_b = iota((ncol, ncol), 1)
-    rank_l = total((c_a // blk == c_b // blk) & (c_a < c_b), present_s, 0)
-    present_l = total(c_a == c_b, present_s, 0)
-    c_l = iota((1, ncol), 1)
-    owner = c_l // blk
-    slot_l = (
-        ((my_y + 2 - owner // 8) % 2) * 8
-        + ((my_x + 4 - (owner // 2) % 4) % 4) * 2
-        + (my_c + 2 - owner % 2) % 2
-    )
-    place_l = slot_l * NEED + jnp.minimum(rank_l, NEED - 1)
     place_s = total(cols_s == c_l, place_l, 1)
-    mine = (slot_l == iota((16, ncol), 0)) & (present_l > 0)
-    wanted = jnp.zeros((16, 128), i32)
-    for k in range(NEED):
-        pick = total(mine & (rank_l == k), c_l % blk, 1)
-        wanted = jnp.where(iota((16, 128), 1) == k, pick, wanted)
-    for d in range(16):
-        meta_out[d] = wanted[d:d + 1, :]
-
     slot_id = iota((slots, 1), 0)
     tab[0:1, 0:slots] = total(place_hot, slot_id, 0)
     tab[1:2, 0:slots] = total(place_hot, place_s, 0)
@@ -118,30 +141,14 @@
 
     tab_copy = pltpu.make_async_copy(tab, tab_sm, tab_sem)
     tab_copy.start()
-    self_copy = pltpu.make_async_copy(meta_out.at[0], meta_sm.at[0], self_sem)
-    self_copy.start()
-
-    pl.semaphore_wait(barrier, n_row - 1)
-
-    def request(d):
-        return pltpu.make_async_remote_copy(
-            src_ref=meta_out.at[d], dst_ref=meta_in.at[d],
-            send_sem=meta_ssem.at[d], recv_sem=meta_rsem.at[d],
-            device_id=peer(NEG[d]), device_id_type=MESH,
-        )
-
-    for d in FAR:
-        request(d).start()
-
-    decay_l = decay_ref[...]
+
+    decay_l = decay_v[...]
     nseed = seeds.shape[0]
     e_sub = lax.broadcasted_iota(i32, (nseed, nseed), 0)
     e_lane = lax.broadcasted_iota(i32, (nseed, nseed), 1)
     decay = jnp.sum(jnp.where(e_sub == e_lane, decay_l, 0.0), axis=1, keepdims=True)
     res[0:nseed, 0:128] = jnp.broadcast_to(decay, (nseed, 128))
 
-    seed_load.wait()
-    tab_copy.wait()
     self_copy.wait()
 
     def exchange(p, d):
@@ -159,25 +166,29 @@
         for k in range(NEED):
             recv[p][k] = own[p, bounded(meta_sm[0, 0, k], blk)]
 
+    seed_load.wait()
     for h in range(HALVES):
         for r in range(blk):
             own[h, r] = seeds[h * half:(h + 1) * half, r * TILE:(r + 1) * TILE].astype(jnp.bfloat16)
     near = FAR[::-1]
+    last = None
     for d in near:
         request(d).wait_recv()
-        to_sm = pltpu.make_async_copy(meta_in.at[d], meta_sm.at[d], asm_sem.at[d])
-        to_sm.start()
-    for d in near:
-        pltpu.make_async_copy(meta_in.at[d], meta_sm.at[d], asm_sem.at[d]).wait()
-    for p in range(HALVES):
-        last = None
-        for d in FAR:
-            fill(p, d)
-            if last is not None:
-                exchange(p, last).start()
-            last = d
-        fill_self(p)
-        exchange(p, last).start()
+        fill(0, d)
+        if last is not None:
+            exchange(0, last).start()
+        last = d
+    fill_self(0)
+    exchange(0, last).start()
+    last = None
+    for d in FAR:
+        fill(1, d)
+        if last is not None:
+            exchange(1, last).start()
+        last = d
+    fill_self(1)
+    exchange(1, last).start()
+    tab_copy.wait()
     for copy in tile_loads:
         copy.wait()
 
@@ -229,7 +240,7 @@
             square = jnp.zeros((half, TILE), f32)
             for r in range(blk):
                 v = value(r)
-                res[rows_h, 128 + r * TILE:128 + (r + 1) * TILE] = v
+                out_ref[rows_h, r * TILE:(r + 1) * TILE] = v
                 square = square + v * v
             energy = jnp.sum(square, axis=1, keepdims=True)
             q_sub = lax.broadcasted_iota(i32, (half, 128), 0)
@@ -239,9 +250,6 @@
             sq_in[h, 0] = flat
             for d in FAR:
                 squares(h, d).start()
-            pltpu.make_async_copy(
-                res.at[rows_h, pl.ds(128, blk * TILE)], out_hbm.at[rows_h, :], out_sem.at[h]
-            ).start()
 
         for d in FAR:
             exchange(p, d).wait_send()
@@ -262,12 +270,12 @@
         acc = sq_in[h, 0]
         for d in range(1, 16):
             acc = acc + sq_in[h, d]
-        norm_ref[h:h + 1, :] = acc
-    for h in range(HALVES):
-        pltpu.make_async_copy(
-            res.at[pl.ds(h * half, half), pl.ds(128, blk * TILE)],
-            out_hbm.at[pl.ds(h * half, half), :], out_sem.at[h],
-        ).wait()
+        hit = iota((half, 128), 0) == iota((half, 128), 1)
+        mean = jnp.sum(jnp.where(hit, acc, 0.0), axis=1, keepdims=True) / (n_row * blk * TILE)
+        scale = 1.0 / jnp.sqrt(mean + 1e-06)
+        for r in range(blk):
+            at = (slice(h * half, (h + 1) * half), slice(r * TILE, (r + 1) * TILE))
+            out_ref[at] = out_ref[at] * scale
 
 
 def per_device(tiles, tile_rows, tile_cols, tile_count, seeds, decay):
@@ -279,16 +287,14 @@
     phases = ITERS * HALVES
     bf16, f32, i32 = jnp.bfloat16, jnp.float32, jnp.int32
     vmem = pl.BlockSpec(memory_space=pltpu.VMEM)
+    smem = pl.BlockSpec(memory_space=pltpu.SMEM)
     anywhere = pl.BlockSpec(memory_space=pl.ANY)
     dma = pltpu.SemaphoreType.DMA
-    iterate, squares = pl.pallas_call(
+    return pl.pallas_call(
         kernel,
-        out_shape=(
-            jax.ShapeDtypeStruct((nseed, width), f32),
-            jax.ShapeDtypeStruct((HALVES, 128), f32),
-        ),
-        in_specs=[anywhere, vmem, vmem, vmem, anywhere, vmem],
-        out_specs=(anywhere, vmem),
+        out_shape=jax.ShapeDtypeStruct((nseed, width), f32),
+        in_specs=[anywhere, anywhere, anywhere, smem, anywhere, anywhere],
+        out_specs=vmem,
         scratch_shapes=[
             pltpu.VMEM((slots, TILE, TILE), bf16),
             pltpu.VMEM((slots, TILE, TILE), bf16),
@@ -297,26 +303,25 @@
             pltpu.VMEM((phases, n_row * NEED, half, TILE), bf16),
             *[pltpu.VMEM((n_row * NEED, half, TILE), bf16) for _ in range(phases)],
             pltpu.VMEM((slots, half, TILE), f32),
-            pltpu.VMEM((nseed, 128 + width), f32),
-            pltpu.VMEM((16, 1, 128), i32),
+            pltpu.VMEM((nseed, 128), f32),
+            pltpu.VMEM((1, slots), i32),
+            pltpu.VMEM((1, slots), i32),
+            pltpu.VMEM((1, nseed), f32),
             pltpu.VMEM((16, 1, 128), i32),
             pltpu.SMEM((16, 1, 128), i32),
             pltpu.VMEM((8, 128), i32),
             pltpu.SMEM((8, 128), i32),
             pltpu.VMEM((HALVES, 1, 128), f32),
             pltpu.VMEM((HALVES, 16, 1, 128), f32),
-            dma((9,)), dma, dma, dma((16,)), dma((16,)), dma((16,)),
-            dma((phases, 16)), dma((phases, 16)), dma((HALVES, 16)), dma((HALVES, 16)), dma((HALVES,)),
+            dma((12,)), dma, dma, dma((16,)), dma((16,)),
+            dma((phases, 16)), dma((phases, 16)), dma((HALVES, 16)), dma((HALVES, 16)),
         ],
         compiler_params=pltpu.CompilerParams(collective_id=0, has_side_effects=True),
         name="katz",
     )(
         tiles, tile_rows.reshape(1, slots), tile_cols.reshape(1, slots),
-        tile_count.reshape(1, 1), seeds, decay.reshape(1, nseed),
+        tile_count, seeds, decay.reshape(1, nseed),
     )
-    total_nodes = n_row * width
-    norm_value = jnp.sqrt(squares[:, :half].reshape(nseed) / total_nodes + 1e-06)
-    return iterate / norm_value[:, None]
 
 
 def solution(mesh):

time: 62.6 us -> 60.8 us (0.971)
  other arithmetic: 2.59 us -> 0 us
  local copies, waits for them, and re-layouts: 0.08 us -> 1.87 us
  Pallas kernels: 58.9 us -> 58.2 us
    div x1 -> x0, other arithmetic: 1.95 us -> none  [per_device(): return iterate / norm_value[:, None]]
    unnamed x0 -> x1, local copies, waits for them, and re-layouts: none -> 1.87 us
    pallas_call x1, Pallas kernels: 58.9 us -> 58.2 us  [per_device(): pl.pallas_call(kernel, out_shape=jax.ShapeDtypeStruct((nseed, width), f32...]
    sqrt x1 -> x0, other arithmetic: 0.64 us -> none  [per_device(): jnp.sqrt(squares[:, :half].reshape(nseed) / total_nodes + 1e-06)]
where the time goes in v2:
time: 60.8 us; the launch traced here: 60.7 us
  Pallas kernels  58.2 us (96%)
  local copies, waits for them, and re-layouts  1.87 us (3%)
  between operations  0.66 us (1%)
    pallas_call x1, Pallas kernels, per_device(): pl.pallas_call(kernel, out_shape=jax.ShapeDtypeStruct((nseed, width), f32...  58.2 us
    unnamed x1, local copies, waits for them, and re-layouts  1.87 us

profile of v2, /device:TPU:1, one launch (start us, length us, event | category | flops | bytes accessed | tf_op | source)
XLA Modules:
  0.0 60.7 jit_solution(14818121378459351538)
XLA Ops:
  0.7 58.2 %katz.1 = f32[32,4096]{1,0:T(8,128)} custom-call(bf16[64,256,256]{2,1,0:T(8,128)(2,1)} %tiles_hbm.1, s32[1,64]{1,0:T(1,128)} %bitcast.3, s32[1,64]{1,0:T(1,128)} %bitcast.4, s32[1]{0:T(128)S(6)} %copy.8.count_ref, f32[32,4096]{1,0:T(8,128)} %seeds_hbm.1, f32[1,32]{1,0:T(1,128)} %bitcast.5), custom_call_target="tpu_custom_call" | custom-call | tf_op jit(solution)/shard_map/katz/pallas_call | solution.py:293
  58.8 1.9 %copy.9 = f32[32,4096]{1,0:T(8,128)} copy(f32[32,4096]{1,0:T(8,128)} %katz.1) | data formatting | bytes 1048576

commit v3 on v2

--- a/solution.py
+++ b/solution.py
@@ -21,14 +21,15 @@
 
 
 FAR = sorted(range(1, 16), key=lambda d: (-hops(d), d))
+MIXED = [13, 3, 7, 5, 9, 11, 15, 2, 6, 4, 12, 8, 10, 14, 1]
 
 
 def kernel(
-    tiles_hbm, rows_hbm, cols_hbm, count_ref, seeds_hbm, decay_hbm,
+    tiles_hbm, rows_hbm, cols_hbm, count_hbm, seeds_hbm, decay_hbm,
     out_ref,
     tiles, tiles_t, seeds, own, sendbuf,
     recv0, recv1, recv2, recv3, recv4, recv5, pref, res,
-    rows_v, cols_v, decay_v, meta_out, meta_sm, tab, tab_sm, sq_out, sq_in,
+    rows_v, cols_v, decay_v, count_s, meta_out, meta_sm, tab, tab_sm, sq_out, sq_in,
     load_sem, tab_sem, self_sem, meta_ssem, meta_rsem,
     ssem, rsem, sq_ssem, sq_rsem,
 ):
@@ -56,7 +57,7 @@
 
     small_loads = [
         pltpu.make_async_copy(src, dst, load_sem.at[9 + i])
-        for i, (src, dst) in enumerate(((cols_hbm, cols_v), (rows_hbm, rows_v), (decay_hbm, decay_v)))
+        for i, (src, dst) in enumerate(((cols_hbm, cols_v), (count_hbm, count_s), (rows_hbm, rows_v), (decay_hbm, decay_v)))
     ]
     for copy in small_loads:
         copy.start()
@@ -83,7 +84,7 @@
 
     ncol = n_row * blk
     cols_l = cols_v[...]
-    live_l = iota((1, slots), 1) < count_ref[0]
+    live_l = iota((1, slots), 1) < count_s[0]
     key_l = jnp.where(live_l, rows_v[...], blk)
     sub = iota((slots, slots), 0)
     lane = iota((slots, slots), 1)
@@ -181,7 +182,7 @@
     fill_self(0)
     exchange(0, last).start()
     last = None
-    for d in FAR:
+    for d in MIXED:
         fill(1, d)
         if last is not None:
             exchange(1, last).start()
@@ -200,7 +201,7 @@
     for d in FAR:
         request(d).wait_send()
 
-    group = 16
+    group = 32
 
     def phase(p):
         h = p % HALVES
@@ -228,7 +229,7 @@
             for r in range(blk):
                 own[nxt, r] = value(r).astype(jnp.bfloat16)
             last = None
-            for d in FAR:
+            for d in MIXED:
                 fill(nxt, d)
                 if last is not None:
                     exchange(nxt, last).start()
@@ -265,8 +266,7 @@
         phase(p)
     for h in range(HALVES):
         for d in FAR:
-            squares(h, d).wait()
-    for h in range(HALVES):
+            squares(h, d).wait_recv()
         acc = sq_in[h, 0]
         for d in range(1, 16):
             acc = acc + sq_in[h, d]
@@ -276,6 +276,9 @@
         for r in range(blk):
             at = (slice(h * half, (h + 1) * half), slice(r * TILE, (r + 1) * TILE))
             out_ref[at] = out_ref[at] * scale
+    for h in range(HALVES):
+        for d in FAR:
+            squares(h, d).wait_send()
 
 
 def per_device(tiles, tile_rows, tile_cols, tile_count, seeds, decay):
@@ -287,13 +290,12 @@
     phases = ITERS * HALVES
     bf16, f32, i32 = jnp.bfloat16, jnp.float32, jnp.int32
     vmem = pl.BlockSpec(memory_space=pltpu.VMEM)
-    smem = pl.BlockSpec(memory_space=pltpu.SMEM)
     anywhere = pl.BlockSpec(memory_space=pl.ANY)
     dma = pltpu.SemaphoreType.DMA
     return pl.pallas_call(
         kernel,
         out_shape=jax.ShapeDtypeStruct((nseed, width), f32),
-        in_specs=[anywhere, anywhere, anywhere, smem, anywhere, anywhere],
+        in_specs=[anywhere, anywhere, anywhere, anywhere, anywhere, anywhere],
         out_specs=vmem,
         scratch_shapes=[
             pltpu.VMEM((slots, TILE, TILE), bf16),
@@ -307,13 +309,14 @@
             pltpu.VMEM((1, slots), i32),
             pltpu.VMEM((1, slots), i32),
             pltpu.VMEM((1, nseed), f32),
+            pltpu.SMEM((1,), i32),
             pltpu.VMEM((16, 1, 128), i32),
             pltpu.SMEM((16, 1, 128), i32),
             pltpu.VMEM((8, 128), i32),
             pltpu.SMEM((8, 128), i32),
             pltpu.VMEM((HALVES, 1, 128), f32),
             pltpu.VMEM((HALVES, 16, 1, 128), f32),
-            dma((12,)), dma, dma, dma((16,)), dma((16,)),
+            dma((13,)), dma, dma, dma((16,)), dma((16,)),
             dma((phases, 16)), dma((phases, 16)), dma((HALVES, 16)), dma((HALVES, 16)),
         ],
         compiler_params=pltpu.CompilerParams(collective_id=0, has_side_effects=True),

time: 60.8 us -> 58.8 us (0.967)
  Pallas kernels: 58.2 us -> 56.2 us
    pallas_call x1, Pallas kernels: 58.2 us -> 56.2 us  [per_device(): pl.pallas_call(kernel, out_shape=jax.ShapeDtypeStruct((nseed, width), f32...]
where the time goes in v3:
time: 58.8 us; the launch traced here: 58.7 us
  Pallas kernels  56.2 us (96%)
  local copies, waits for them, and re-layouts  1.87 us (3%)
  between operations  0.66 us (1%)
    pallas_call x1, Pallas kernels, per_device(): pl.pallas_call(kernel, out_shape=jax.ShapeDtypeStruct((nseed, width), f32...  56.2 us
    unnamed x1, local copies, waits for them, and re-layouts  1.87 us

profile of v3, /device:TPU:1, one launch (start us, length us, event | category | flops | bytes accessed | tf_op | source)
XLA Modules:
  0.0 58.7 jit_solution(15651276111248569902)
XLA Ops:
  0.7 56.2 %katz.1 = f32[32,4096]{1,0:T(8,128)} custom-call(bf16[64,256,256]{2,1,0:T(8,128)(2,1)} %tiles_hbm.1, s32[1,64]{1,0:T(1,128)} %bitcast.3, s32[1,64]{1,0:T(1,128)} %bitcast.4, s32[1]{0:T(128)S(6)} %copy.8.count_hbm, f32[32,4096]{1,0:T(8,128)} %seeds_hbm.1, f32[1,32]{1,0:T(1,128)} %bitcast.5), custom_call_target="tpu_custom_call" | custom-call | tf_op jit(solution)/shard_map/katz/pallas_call | solution.py:295
  56.8 1.9 %copy.9 = f32[32,4096]{1,0:T(8,128)} copy(f32[32,4096]{1,0:T(8,128)} %katz.1) | data formatting | bytes 1048576

commit v4 on v3

--- a/solution.py
+++ b/solution.py
@@ -25,11 +25,11 @@
 
 
 def kernel(
-    tiles_hbm, rows_hbm, cols_hbm, count_hbm, seeds_hbm, decay_hbm,
+    tiles_hbm, rows_ref, cols_ref, count_ref, seeds_hbm, decay_ref,
     out_ref,
     tiles, tiles_t, seeds, own, sendbuf,
     recv0, recv1, recv2, recv3, recv4, recv5, pref, res,
-    rows_v, cols_v, decay_v, count_s, meta_out, meta_sm, tab, tab_sm, sq_out, sq_in,
+    meta_out, meta_sm, tab, tab_sm, sq_out, sq_in,
     load_sem, tab_sem, self_sem, meta_ssem, meta_rsem,
     ssem, rsem, sq_ssem, sq_rsem,
 ):
@@ -55,12 +55,6 @@
     for d in FAR:
         pl.semaphore_signal(barrier, inc=1, device_id=peer(d), device_id_type=MESH)
 
-    small_loads = [
-        pltpu.make_async_copy(src, dst, load_sem.at[9 + i])
-        for i, (src, dst) in enumerate(((cols_hbm, cols_v), (count_hbm, count_s), (rows_hbm, rows_v), (decay_hbm, decay_v)))
-    ]
-    for copy in small_loads:
-        copy.start()
     seed_load = pltpu.make_async_copy(seeds_hbm, seeds, load_sem.at[8])
     seed_load.start()
     part = slots // 8
@@ -71,8 +65,6 @@
     for copy in tile_loads:
         copy.start()
 
-    for copy in small_loads:
-        copy.wait()
     f32 = jnp.float32
     i32 = jnp.int32
 
@@ -83,9 +75,9 @@
         return jnp.sum(jnp.where(hit, v, 0), axis=axis, keepdims=True)
 
     ncol = n_row * blk
-    cols_l = cols_v[...]
-    live_l = iota((1, slots), 1) < count_s[0]
-    key_l = jnp.where(live_l, rows_v[...], blk)
+    cols_l = cols_ref[...]
+    live_l = iota((1, slots), 1) < count_ref[0]
+    key_l = jnp.where(live_l, rows_ref[...], blk)
     sub = iota((slots, slots), 0)
     lane = iota((slots, slots), 1)
     cols_s = total(sub == lane, cols_l, 1)
@@ -143,7 +135,7 @@
     tab_copy = pltpu.make_async_copy(tab, tab_sm, tab_sem)
     tab_copy.start()
 
-    decay_l = decay_v[...]
+    decay_l = decay_ref[...]
     nseed = seeds.shape[0]
     e_sub = lax.broadcasted_iota(i32, (nseed, nseed), 0)
     e_lane = lax.broadcasted_iota(i32, (nseed, nseed), 1)
@@ -201,7 +193,7 @@
     for d in FAR:
         request(d).wait_send()
 
-    group = 32
+    group = 64
 
     def phase(p):
         h = p % HALVES
@@ -290,12 +282,13 @@
     phases = ITERS * HALVES
     bf16, f32, i32 = jnp.bfloat16, jnp.float32, jnp.int32
     vmem = pl.BlockSpec(memory_space=pltpu.VMEM)
-    anywhere = pl.BlockSpec(memory_space=pl.ANY)
+    smem = pl.BlockSpec(memory_space=pltpu.SMEM)
+    outside = pl.BlockSpec(memory_space=pltpu.HBM)
     dma = pltpu.SemaphoreType.DMA
     return pl.pallas_call(
         kernel,
         out_shape=jax.ShapeDtypeStruct((nseed, width), f32),
-        in_specs=[anywhere, anywhere, anywhere, anywhere, anywhere, anywhere],
+        in_specs=[outside, vmem, vmem, smem, outside, vmem],
         out_specs=vmem,
         scratch_shapes=[
             pltpu.VMEM((slots, TILE, TILE), bf16),
@@ -306,20 +299,18 @@
             *[pltpu.VMEM((n_row * NEED, half, TILE), bf16) for _ in range(phases)],
             pltpu.VMEM((slots, half, TILE), f32),
             pltpu.VMEM((nseed, 128), f32),
-            pltpu.VMEM((1, slots), i32),
-            pltpu.VMEM((1, slots), i32),
-            pltpu.VMEM((1, nseed), f32),
-            pltpu.SMEM((1,), i32),
             pltpu.VMEM((16, 1, 128), i32),
             pltpu.SMEM((16, 1, 128), i32),
             pltpu.VMEM((8, 128), i32),
             pltpu.SMEM((8, 128), i32),
             pltpu.VMEM((HALVES, 1, 128), f32),
             pltpu.VMEM((HALVES, 16, 1, 128), f32),
-            dma((13,)), dma, dma, dma((16,)), dma((16,)),
+            dma((9,)), dma, dma, dma((16,)), dma((16,)),
             dma((phases, 16)), dma((phases, 16)), dma((HALVES, 16)), dma((HALVES, 16)),
         ],
-        compiler_params=pltpu.CompilerParams(collective_id=0, has_side_effects=True),
+        compiler_params=pltpu.CompilerParams(
+            collective_id=0, has_side_effects=True, vmem_limit_bytes=53 * 2**20
+        ),
         name="katz",
     )(
         tiles, tile_rows.reshape(1, slots), tile_cols.reshape(1, slots),

time: 58.8 us -> 58.5 us (level)
  Pallas kernels: 56.2 us -> 55 us
  local copies, waits for them, and re-layouts: 1.87 us -> 2.75 us
    pallas_call x1, Pallas kernels: 56.2 us -> 55 us  [per_device(): pl.pallas_call(kernel, out_shape=jax.ShapeDtypeStruct((nseed, width), f32...]
    unnamed x1 -> x7, local copies, waits for them, and re-layouts: 1.87 us -> 2.75 us
where the time goes in v4:
time: 58.5 us; the launch traced here: 58.4 us
  Pallas kernels  55 us (94%)
  local copies, waits for them, and re-layouts  2.75 us (5%)
  between operations  0.67 us (1%)
    pallas_call x1, Pallas kernels, per_device(): pl.pallas_call(kernel, out_shape=jax.ShapeDtypeStruct((nseed, width), f32...  55 us
    unnamed x7, local copies, waits for them, and re-layouts  2.75 us

profile of v4, /device:TPU:1, one launch (start us, length us, event | category | flops | bytes accessed | tf_op | source)
XLA Modules:
  0.0 58.4 jit_solution(11021070934290534291)
XLA Ops:
  0.7 0.0 copy-start
  0.7 0.6 %copy-done = s32[64]{0:T(128)S(1)} copy-done((s32[64]{0:T(128)S(1)}, s32[64]{0:T(128)}, u32[]{:S(2)}) %copy-start) | copy-done | bytes 280
  1.3 0.0 copy-start.1
  1.3 0.7 %copy-done.1 = s32[64]{0:T(128)S(1)} copy-done((s32[64]{0:T(128)S(1)}, s32[64]{0:T(128)}, u32[]{:S(2)}) %copy-start.1) | copy-done | bytes 280
  2.0 0.0 copy-start.2
  2.0 0.7 %copy-done.2 = f32[32]{0:T(128)S(1)} copy-done((f32[32]{0:T(128)S(1)}, f32[32]{0:T(128)}, u32[]{:S(2)}) %copy-start.2) | copy-done | bytes 152
  2.6 55.0 %katz.1 = f32[32,4096]{1,0:T(8,128)S(1)} custom-call(bf16[64,256,256]{2,1,0:T(8,128)(2,1)} %tiles_hbm.1, s32[1,64]{1,0:T(1,128)S(1)} %bitcast.3, s32[1,64]{1,0:T(1,128)S(1)} %bitcast.4, s32[1]{0:T(128)S(6)} %copy.8.count_ref, f32[32,4096]{1,0:T(8,128)} %seeds_hbm.1, f32[1,32]{1,0:T(1,128)S(1)} %bitcast.5), custom_call_target="tpu_custom_call" | custom-call | tf_op jit(solution)/shard_map/katz/pallas_call | solution.py:288
  57.6 0.8 %copy.9 = f32[32,4096]{1,0:T(8,128)} copy(f32[32,4096]{1,0:T(8,128)S(1)} %katz.1) | data formatting | bytes 1048576
Async XLA Ops:
  0.7 0.7 %copy-start = (s32[64]{0:T(128)S(1)}, s32[64]{0:T(128)}, u32[]{:S(2)}) copy-start(s32[64]{0:T(128)} %param.7) | copy-start | bytes 772
  1.3 0.7 %copy-start.1 = (s32[64]{0:T(128)S(1)}, s32[64]{0:T(128)}, u32[]{:S(2)}) copy-start(s32[64]{0:T(128)} %param.8) | copy-start | bytes 772
  2.0 0.7 %copy-start.2 = (f32[32]{0:T(128)S(1)}, f32[32]{0:T(128)}, u32[]{:S(2)}) copy-start(f32[32]{0:T(128)} %param.11) | copy-start | bytes 388
